TPU v7x, 512 devices: a whole 4x8x8 slice. The times are simulated.
512 devices in a mesh: section: 8 (over y_hi, core), dp: 64 (over x, y_lo, z).
Axes of the slice: x: 4, y: 8 (y_hi: 4, y_lo: 2; y = y_hi * 2 + y_lo), z: 8, core: 2. Of those that a mesh axis runs over, the one named last changes fastest.
Arguments:
- node_table: bfloat16 [128, 2048], replicated, may hold values from -60 to 60
- tiles: int32 [4, 2048], P(None, 'dp'), may hold values from 0 to 96
- neighbours: int32 [4, 2048, 8], P(None, 'dp'), may hold values from 0 to 31
- distances: float32 [4, 2048, 8], P(None, 'dp'), may hold values from 0 to 0.9
- proj: bfloat16 [8, 2048, 512], P('section'), may hold values from -0.125 to 0.125
- upstream: bfloat16 [4, 2048, 2048], P(None, 'dp'), may hold values from -16 to 16
Outputs:
- grad: float32 [8, 2048, 512], P('section', 'dp')
All inputs are finite; a program needn't handle non-finite values.
Results may differ from a plain program's by a relative error of at most 0.024.
Values may be sent and summed in bfloat16 or wider, within the bound.
A program may use at most 64 MiB of HBM per device.

v0:
```python
import math

import jax
import jax.numpy as jnp
from jax import lax
from jax.sharding import Mesh
from jax.sharding import PartitionSpec as P

DP = ("dp_0", "dp_1", "dp_2")


epsilon = 1e-05


def from_behind(block, axis, distance):
    devices = range(lax.axis_size(axis))
    route = [(i - distance, i) for i in devices if i - distance in devices]
    return lax.ppermute(block, axis, route)


def reduced_to_own(pieces, axes, turns):
    inside = pieces.shape[1:]
    pieces = pieces.reshape(*(lax.axis_size(a) for a in axes), *inside)
    pieces = jnp.moveaxis(pieces, turns, range(len(axes))).reshape(-1, *inside)
    for k in turns:
        pieces = lax.psum_scatter(pieces, axes[k], scatter_dimension=0, tiled=True)
    return pieces[0]


def split_up(shard, dim, size):
    lengths = shard.shape
    pieces = shard.reshape(*lengths[:dim], size, lengths[dim] // size, *lengths[dim + 1 :])
    return jnp.moveaxis(pieces, dim, 0)


def sum_by_axis(shard, axes, turns, dim):
    size = lax.axis_size(axes)
    return reduced_to_own(split_up(shard, dim, size), axes, turns)


def normalize(stream):
    wide = stream.astype(jnp.float32)
    inv_rms = lax.rsqrt(jnp.mean(wide * wide, axis=-1, keepdims=True) + epsilon)
    return (wide * inv_rms, inv_rms)


def contract_rows(left, right):
    return lax.dot_general(
        left, right, (((0,), (0,)), ((), ())), preferred_element_type=jnp.float32
    )


def contract_last(left, right):
    return lax.dot_general(
        left, right, (((1,), (1,)), ((), ())), preferred_element_type=jnp.float32
    )


def put_row(buffer, value, micro_slot, active):
    previous = lax.dynamic_index_in_dim(buffer, micro_slot, 0, keepdims=False)
    return lax.dynamic_update_index_in_dim(
        buffer, jnp.where(active, value, previous), micro_slot, 0
    )


def branch_of(normed, weight):
    return jnp.tanh(jnp.dot(normed, weight, preferred_element_type=jnp.float32)).astype(
        jnp.bfloat16
    )


def on_device(node_table, tiles, neighbours, distances, proj, upstream):
    section_count = lax.axis_size("section")
    section_index = lax.axis_index("section")
    micro_count, row_count = tiles.shape
    node_count, width = node_table.shape
    weight = proj[0]
    rank_width = weight.shape[1]
    kernel = (1.0 - distances) ** 3 * (1.0 + 3.0 * distances)
    weight_sum = jnp.sum(kernel, axis=-1, keepdims=True)
    node_index = tiles[:, :, None] + neighbours
    onehot = (node_index[..., None] == jnp.arange(node_count, dtype=jnp.int32)).astype(jnp.float32)
    selector = (jnp.sum(onehot * kernel[..., None], axis=2) / weight_sum).reshape(-1, node_count)
    select_high = selector.astype(jnp.bfloat16)
    select_low = (selector - select_high.astype(jnp.float32)).astype(jnp.bfloat16)
    first_inputs = jnp.dot(select_high, node_table, preferred_element_type=jnp.float32) + jnp.dot(
        select_low, node_table, preferred_element_type=jnp.float32
    )
    first_inputs = first_inputs.reshape(micro_count, row_count, width).astype(jnp.bfloat16)
    tick_total = micro_count + section_count - 1
    zero_rows = jnp.zeros((row_count, width), jnp.bfloat16)
    stored = jnp.zeros((micro_count, row_count, width), jnp.bfloat16)
    stored_hidden = jnp.zeros((micro_count, row_count, rank_width), jnp.bfloat16)

    def forward_tick(tick_index, loop_state):
        arriving, stored, stored_hidden = loop_state
        micro_slot = tick_index - section_index
        active = (micro_slot >= 0) & (micro_slot < micro_count)
        clamped = jnp.clip(micro_slot, 0, micro_count - 1)
        fresh = lax.dynamic_index_in_dim(first_inputs, clamped, 0, keepdims=False)
        stream = jnp.where(section_index == 0, fresh, arriving)
        wide, inv_rms = normalize(stream)
        hidden = branch_of(wide.astype(jnp.bfloat16), weight)
        leaving = (stream.astype(jnp.float32) + contract_last(hidden, weight)).astype(jnp.bfloat16)
        stored = put_row(stored, stream, clamped, active)
        arriving = from_behind(leaving, "section", 1)
        return (arriving, stored, stored_hidden)

    _, stored, stored_hidden = lax.fori_loop(
        0, tick_total, forward_tick, (zero_rows, stored, stored_hidden)
    )
    grad_store = jnp.zeros((micro_count, row_count, width), jnp.bfloat16)
    act_store = jnp.zeros((micro_count, row_count, rank_width), jnp.bfloat16)

    def backward_tick(tick_index, loop_state):
        arriving, grad_store, act_store = loop_state
        micro_slot = tick_index - (section_count - 1 - section_index)
        active = (micro_slot >= 0) & (micro_slot < micro_count)
        clamped = jnp.clip(micro_slot, 0, micro_count - 1)
        fresh = lax.dynamic_index_in_dim(upstream, clamped, 0, keepdims=False)
        cotangent = jnp.where(section_index == section_count - 1, fresh, arriving)
        stream = lax.dynamic_index_in_dim(stored, clamped, 0, keepdims=False)
        wide, inv_rms = normalize(stream)
        hidden = branch_of(wide.astype(jnp.bfloat16), weight)
        hidden_wide = hidden.astype(jnp.float32)
        grad_hidden = jnp.dot(cotangent, weight, preferred_element_type=jnp.float32)
        grad_act = (grad_hidden * (1.0 - hidden_wide * hidden_wide)).astype(jnp.bfloat16)
        grad_norm = contract_last(grad_act, weight)
        correction = jnp.mean(grad_norm * wide, axis=-1, keepdims=True)
        leaving = (
            cotangent.astype(jnp.float32) + inv_rms * (grad_norm - wide * correction)
        ).astype(jnp.bfloat16)
        grad_store = put_row(grad_store, cotangent, clamped, active)
        act_store = put_row(act_store, grad_act, clamped, active)
        arriving = from_behind(leaving, "section", -1)
        return (arriving, grad_store, act_store)

    _, grad_store, act_store = lax.fori_loop(
        0, tick_total, backward_tick, (zero_rows, grad_store, act_store)
    )
    flat_wide, flat_inv = normalize(stored.reshape(-1, width))
    flat_normed = flat_wide.astype(jnp.bfloat16)
    flat_hidden = branch_of(flat_normed, weight)
    local_grad = contract_rows(flat_normed, act_store.reshape(-1, rank_width)) + contract_rows(
        grad_store.reshape(-1, width), flat_hidden
    )
    replica_count = lax.axis_size(DP)
    factor = 1.0 / math.sqrt(micro_count * row_count * replica_count)
    share = sum_by_axis(local_grad, DP, (0, 2, 1), 0)
    return (share * factor)[None]


def solution(mesh):
    finer = Mesh(
        mesh.devices.reshape(mesh.shape["section"], 4, 2, 8), ("section", "dp_0", "dp_1", "dp_2")
    )
    in_specs = (
        P(),
        P(None, DP),
        P(None, DP, None),
        P(None, DP, None),
        P("section", None, None),
        P(None, DP, None),
    )
    out_specs = P("section", DP, None)
    return jax.shard_map(
        on_device, mesh=finer, in_specs=in_specs, out_specs=out_specs, check_vma=False
    )
```

profile of v0, /device:TPU:1, one launch (start us, length us, event | category | flops | bytes accessed | tf_op | source)
XLA Modules:
  0.0 431.8 jit_solution(14136465161337104227)
XLA Ops:
  10.4 112.0 %while.35 = (s32[]{:T(128)}, bf16[32,2048]{1,0:T(8,128)(2,1)S(1)}, bf16[4,32,2048]{2,1,0:T(8,128)(2,1)S(1)}, pred[]{:T(512)}, s32[]{:T(128)}, /*index=5*/bf16[4,...) while((s32[]{:T(128)}, bf16[32,2048]{1,0:T(8,128)(2,1)S(1)}, ...), condition=%wide.region_4.5_spmd, body=%wide.region_2.4_spmd.sunk | while | flops 134955040 | bytes 3932888 | solution.py:109
  12.7 5.6 %collective-permute-start = (bf16[32,2048]{1,0:T(8,128)(2,1)S(1)}, bf16[32,2048]{1,0:T(8,128)(2,1)S(1)}, u32[]{:S(2)}, u32[]{:S(2)}) collective-permute-start(bf16[32,2048]{1,0:T(8,128)(2,1)S(1)} %fusion.71), channel_id=1, source_target_pairs={{0,64},{64,128},{128,192},{192,256},{256,320},{320,384},{384,448},... | collective-permute-start | bytes 393224 | tf_op jit(solution)/shard_map/while/body/eval_jaxpr/ppermute | solution.py:18
  60.7 6.3 %collective-permute-start = (bf16[32,2048]{1,0:T(8,128)(2,1)S(1)}, bf16[32,2048]{1,0:T(8,128)(2,1)S(1)}, u32[]{:S(2)}, u32[]{:S(2)}) collective-permute-start(bf16[32,2048]{1,0:T(8,128)(2,1)S(1)} %fusion.71), channel_id=1, source_target_pairs={{0,64},{64,128},{128,192},{192,256},{256,320},{320,384},{384,448},... | collective-permute-start | bytes 393224 | tf_op jit(solution)/shard_map/while/body/eval_jaxpr/ppermute | solution.py:18
  71.3 6.5 %collective-permute-start = (bf16[32,2048]{1,0:T(8,128)(2,1)S(1)}, bf16[32,2048]{1,0:T(8,128)(2,1)S(1)}, u32[]{:S(2)}, u32[]{:S(2)}) collective-permute-start(bf16[32,2048]{1,0:T(8,128)(2,1)S(1)} %fusion.71), channel_id=1, source_target_pairs={{0,64},{64,128},{128,192},{192,256},{256,320},{320,384},{384,448},... | collective-permute-start | bytes 393224 | tf_op jit(solution)/shard_map/while/body/eval_jaxpr/ppermute | solution.py:18
  82.0 6.5 %collective-permute-start = (bf16[32,2048]{1,0:T(8,128)(2,1)S(1)}, bf16[32,2048]{1,0:T(8,128)(2,1)S(1)}, u32[]{:S(2)}, u32[]{:S(2)}) collective-permute-start(bf16[32,2048]{1,0:T(8,128)(2,1)S(1)} %fusion.71), channel_id=1, source_target_pairs={{0,64},{64,128},{128,192},{192,256},{256,320},{320,384},{384,448},... | collective-permute-start | bytes 393224 | tf_op jit(solution)/shard_map/while/body/eval_jaxpr/ppermute | solution.py:18
  92.7 6.5 %collective-permute-start = (bf16[32,2048]{1,0:T(8,128)(2,1)S(1)}, bf16[32,2048]{1,0:T(8,128)(2,1)S(1)}, u32[]{:S(2)}, u32[]{:S(2)}) collective-permute-start(bf16[32,2048]{1,0:T(8,128)(2,1)S(1)} %fusion.71), channel_id=1, source_target_pairs={{0,64},{64,128},{128,192},{192,256},{256,320},{320,384},{384,448},... | collective-permute-start | bytes 393224 | tf_op jit(solution)/shard_map/while/body/eval_jaxpr/ppermute | solution.py:18
  103.4 6.5 %collective-permute-start = (bf16[32,2048]{1,0:T(8,128)(2,1)S(1)}, bf16[32,2048]{1,0:T(8,128)(2,1)S(1)}, u32[]{:S(2)}, u32[]{:S(2)}) collective-permute-start(bf16[32,2048]{1,0:T(8,128)(2,1)S(1)} %fusion.71), channel_id=1, source_target_pairs={{0,64},{64,128},{128,192},{192,256},{256,320},{320,384},{384,448},... | collective-permute-start | bytes 393224 | tf_op jit(solution)/shard_map/while/body/eval_jaxpr/ppermute | solution.py:18
  114.1 6.5 %collective-permute-start = (bf16[32,2048]{1,0:T(8,128)(2,1)S(1)}, bf16[32,2048]{1,0:T(8,128)(2,1)S(1)}, u32[]{:S(2)}, u32[]{:S(2)}) collective-permute-start(bf16[32,2048]{1,0:T(8,128)(2,1)S(1)} %fusion.71), channel_id=1, source_target_pairs={{0,64},{64,128},{128,192},{192,256},{256,320},{320,384},{384,448},... | collective-permute-start | bytes 393224 | tf_op jit(solution)/shard_map/while/body/eval_jaxpr/ppermute | solution.py:18
  125.2 160.4 %while.36 = (s32[]{:T(128)}, bf16[32,2048]{1,0:T(8,128)(2,1)S(1)}, bf16[4,32,2048]{2,1,0:T(8,128)(2,1)}, bf16[4,32,512]{2,1,0:T(8,128)(2,1)}, pred[]{:T(512)}, /...) while((s32[]{:T(128)}, bf16[32,2048]{1,0:T(8,128)(2,1)S(1)}, ...), condition=%wide.region_9.10_spmd, body=%wide.region_6.9_spmd.sunk | while | flops 202752032 | bytes 9505152 | solution.py:138
  133.1 8.6 %collective-permute-done.1 = bf16[32,2048]{1,0:T(8,128)(2,1)S(1)} collective-permute-done((bf16[32,2048]{1,0:T(8,128)(2,1)S(1)}, bf16[32,2048]{1,0:T(8,128)(2,1)S(1)}, u32[]{:S(2)}, u32[]{:S(2)}) %collective-permute-start.1) | collective-permute-done | bytes 131104 | tf_op jit(solution)/shard_map/while/body/eval_jaxpr/ppermute | solution.py:18
  149.7 6.5 %collective-permute-done.1 = bf16[32,2048]{1,0:T(8,128)(2,1)S(1)} collective-permute-done((bf16[32,2048]{1,0:T(8,128)(2,1)S(1)}, bf16[32,2048]{1,0:T(8,128)(2,1)S(1)}, u32[]{:S(2)}, u32[]{:S(2)}) %collective-permute-start.1) | collective-permute-done | bytes 131104 | tf_op jit(solution)/shard_map/while/body/eval_jaxpr/ppermute | solution.py:18
  164.1 6.1 %collective-permute-done.1 = bf16[32,2048]{1,0:T(8,128)(2,1)S(1)} collective-permute-done((bf16[32,2048]{1,0:T(8,128)(2,1)S(1)}, bf16[32,2048]{1,0:T(8,128)(2,1)S(1)}, u32[]{:S(2)}, u32[]{:S(2)}) %collective-permute-start.1) | collective-permute-done | bytes 131104 | tf_op jit(solution)/shard_map/while/body/eval_jaxpr/ppermute | solution.py:18
  178.1 6.5 %collective-permute-done.1 = bf16[32,2048]{1,0:T(8,128)(2,1)S(1)} collective-permute-done((bf16[32,2048]{1,0:T(8,128)(2,1)S(1)}, bf16[32,2048]{1,0:T(8,128)(2,1)S(1)}, u32[]{:S(2)}, u32[]{:S(2)}) %collective-permute-start.1) | collective-permute-done | bytes 131104 | tf_op jit(solution)/shard_map/while/body/eval_jaxpr/ppermute | solution.py:18
  192.5 6.5 %collective-permute-done.1 = bf16[32,2048]{1,0:T(8,128)(2,1)S(1)} collective-permute-done((bf16[32,2048]{1,0:T(8,128)(2,1)S(1)}, bf16[32,2048]{1,0:T(8,128)(2,1)S(1)}, u32[]{:S(2)}, u32[]{:S(2)}) %collective-permute-start.1) | collective-permute-done | bytes 131104 | tf_op jit(solution)/shard_map/while/body/eval_jaxpr/ppermute | solution.py:18
  206.9 6.5 %collective-permute-done.1 = bf16[32,2048]{1,0:T(8,128)(2,1)S(1)} collective-permute-done((bf16[32,2048]{1,0:T(8,128)(2,1)S(1)}, bf16[32,2048]{1,0:T(8,128)(2,1)S(1)}, u32[]{:S(2)}, u32[]{:S(2)}) %collective-permute-start.1) | collective-permute-done | bytes 131104 | tf_op jit(solution)/shard_map/while/body/eval_jaxpr/ppermute | solution.py:18
  221.4 6.5 %collective-permute-done.1 = bf16[32,2048]{1,0:T(8,128)(2,1)S(1)} collective-permute-done((bf16[32,2048]{1,0:T(8,128)(2,1)S(1)}, bf16[32,2048]{1,0:T(8,128)(2,1)S(1)}, u32[]{:S(2)}, u32[]{:S(2)}) %collective-permute-start.1) | collective-permute-done | bytes 131104 | tf_op jit(solution)/shard_map/while/body/eval_jaxpr/ppermute | solution.py:18
  235.8 6.5 %collective-permute-done.1 = bf16[32,2048]{1,0:T(8,128)(2,1)S(1)} collective-permute-done((bf16[32,2048]{1,0:T(8,128)(2,1)S(1)}, bf16[32,2048]{1,0:T(8,128)(2,1)S(1)}, u32[]{:S(2)}, u32[]{:S(2)}) %collective-permute-start.1) | collective-permute-done | bytes 131104 | tf_op jit(solution)/shard_map/while/body/eval_jaxpr/ppermute | solution.py:18
  250.2 6.5 %collective-permute-done.1 = bf16[32,2048]{1,0:T(8,128)(2,1)S(1)} collective-permute-done((bf16[32,2048]{1,0:T(8,128)(2,1)S(1)}, bf16[32,2048]{1,0:T(8,128)(2,1)S(1)}, u32[]{:S(2)}, u32[]{:S(2)}) %collective-permute-start.1) | collective-permute-done | bytes 131104 | tf_op jit(solution)/shard_map/while/body/eval_jaxpr/ppermute | solution.py:18
  264.7 6.5 %collective-permute-done.1 = bf16[32,2048]{1,0:T(8,128)(2,1)S(1)} collective-permute-done((bf16[32,2048]{1,0:T(8,128)(2,1)S(1)}, bf16[32,2048]{1,0:T(8,128)(2,1)S(1)}, u32[]{:S(2)}, u32[]{:S(2)}) %collective-permute-start.1) | collective-permute-done | bytes 131104 | tf_op jit(solution)/shard_map/while/body/eval_jaxpr/ppermute | solution.py:18
  279.1 6.5 %collective-permute-done.1 = bf16[32,2048]{1,0:T(8,128)(2,1)S(1)} collective-permute-done((bf16[32,2048]{1,0:T(8,128)(2,1)S(1)}, bf16[32,2048]{1,0:T(8,128)(2,1)S(1)}, u32[]{:S(2)}, u32[]{:S(2)}) %collective-permute-start.1) | collective-permute-done | bytes 131104 | tf_op jit(solution)/shard_map/while/body/eval_jaxpr/ppermute | solution.py:18
  289.3 5.4 %bitcast_add_fusion = f32[2048,512]{1,0:T(8,128)} fusion(f32[2048,512,1]{1,0,2:T(8,128)} %fusion.38, bf16[128,2048]{1,0:T(8,128)(2,1)S(1)} %bitcast.99, bf16[128,2048]{1,0:T(8,128)(2,1)} %bitcast.101, bf16[1,2048,512]{2,1,0:T(8,128)(2,1)S(1)} %bitcast.96), kind=kOutput, calls=%fused_computation.45 | convolution fusion | flops 537985024 | bytes 11534336 | tf_op jit(solution)/shard_map/dot_general | solution.py:48
  299.8 59.9 %reduce-scatter.4.cloned.1.call-done = f32[16,32,512]{2,1,0:T(8,128)} async-done(((f32[64,32,512]{2,1,0:T(8,128)}), f32[16,32,512]{2,1,0:T(8,128)}) %reduce-scatter.4.cloned.1.call-update) | async-done | bytes 1048592 | tf_op jit(solution)/shard_map/reduce_scatter | solution.py:26
  359.8 40.6 %reduce-scatter.6.cloned.1.call-done = f32[2,32,512]{2,1,0:T(8,128)} async-done(((f32[16,32,512]{2,1,0:T(8,128)}), f32[2,32,512]{2,1,0:T(8,128)}) %reduce-scatter.6.cloned.1.call-update) | async-done | bytes 131088 | tf_op jit(solution)/shard_map/reduce_scatter | solution.py:26
  400.4 23.4 %reduce-scatter.8.cloned.1.call-done = f32[1,32,512]{2,1,0:T(8,128)} async-done(((f32[2,32,512]{2,1,0:T(8,128)}), f32[1,32,512]{2,1,0:T(8,128)}) %reduce-scatter.8.cloned.1.call-update) | async-done | bytes 65552 | tf_op jit(solution)/shard_map/reduce_scatter | solution.py:26
  (223 shorter events, 171.4 us)
Async XLA Ops:
  6.5 353.2 %reduce-scatter.4.cloned.1.call-start = ((), (), s32[]{:S(2)}) async-start(), calls=%async_computation.3 | async-start | bytes 5242880 | tf_op jit(solution)/shard_map/reduce_scatter | solution.py:26
  12.7 9.0 %collective-permute-start = (bf16[32,2048]{1,0:T(8,128)(2,1)S(1)}, bf16[32,2048]{1,0:T(8,128)(2,1)S(1)}, u32[]{:S(2)}, u32[]{:S(2)}) collective-permute-start(bf16[32,2048]{1,0:T(8,128)(2,1)S(1)} %fusion.71), channel_id=1, source_target_pairs={{0,64},{64,128},{128,192},{192,256},{256,320},{320,384},{384,448},... | collective-permute-start | bytes 393224 | tf_op jit(solution)/shard_map/while/body/eval_jaxpr/ppermute | solution.py:18
  32.2 7.2 %collective-permute-start = (bf16[32,2048]{1,0:T(8,128)(2,1)S(1)}, bf16[32,2048]{1,0:T(8,128)(2,1)S(1)}, u32[]{:S(2)}, u32[]{:S(2)}) collective-permute-start(bf16[32,2048]{1,0:T(8,128)(2,1)S(1)} %fusion.71), channel_id=1, source_target_pairs={{0,64},{64,128},{128,192},{192,256},{256,320},{320,384},{384,448},... | collective-permute-start | bytes 393224 | tf_op jit(solution)/shard_map/while/body/eval_jaxpr/ppermute | solution.py:18
  41.7 7.2 %collective-permute-start = (bf16[32,2048]{1,0:T(8,128)(2,1)S(1)}, bf16[32,2048]{1,0:T(8,128)(2,1)S(1)}, u32[]{:S(2)}, u32[]{:S(2)}) collective-permute-start(bf16[32,2048]{1,0:T(8,128)(2,1)S(1)} %fusion.71), channel_id=1, source_target_pairs={{0,64},{64,128},{128,192},{192,256},{256,320},{320,384},{384,448},... | collective-permute-start | bytes 393224 | tf_op jit(solution)/shard_map/while/body/eval_jaxpr/ppermute | solution.py:18
  51.2 7.2 %collective-permute-start = (bf16[32,2048]{1,0:T(8,128)(2,1)S(1)}, bf16[32,2048]{1,0:T(8,128)(2,1)S(1)}, u32[]{:S(2)}, u32[]{:S(2)}) collective-permute-start(bf16[32,2048]{1,0:T(8,128)(2,1)S(1)} %fusion.71), channel_id=1, source_target_pairs={{0,64},{64,128},{128,192},{192,256},{256,320},{320,384},{384,448},... | collective-permute-start | bytes 393224 | tf_op jit(solution)/shard_map/while/body/eval_jaxpr/ppermute | solution.py:18
  60.7 8.3 %collective-permute-start = (bf16[32,2048]{1,0:T(8,128)(2,1)S(1)}, bf16[32,2048]{1,0:T(8,128)(2,1)S(1)}, u32[]{:S(2)}, u32[]{:S(2)}) collective-permute-start(bf16[32,2048]{1,0:T(8,128)(2,1)S(1)} %fusion.71), channel_id=1, source_target_pairs={{0,64},{64,128},{128,192},{192,256},{256,320},{320,384},{384,448},... | collective-permute-start | bytes 393224 | tf_op jit(solution)/shard_map/while/body/eval_jaxpr/ppermute | solution.py:18
  71.3 8.4 %collective-permute-start = (bf16[32,2048]{1,0:T(8,128)(2,1)S(1)}, bf16[32,2048]{1,0:T(8,128)(2,1)S(1)}, u32[]{:S(2)}, u32[]{:S(2)}) collective-permute-start(bf16[32,2048]{1,0:T(8,128)(2,1)S(1)} %fusion.71), channel_id=1, source_target_pairs={{0,64},{64,128},{128,192},{192,256},{256,320},{320,384},{384,448},... | collective-permute-start | bytes 393224 | tf_op jit(solution)/shard_map/while/body/eval_jaxpr/ppermute | solution.py:18
  82.0 8.4 %collective-permute-start = (bf16[32,2048]{1,0:T(8,128)(2,1)S(1)}, bf16[32,2048]{1,0:T(8,128)(2,1)S(1)}, u32[]{:S(2)}, u32[]{:S(2)}) collective-permute-start(bf16[32,2048]{1,0:T(8,128)(2,1)S(1)} %fusion.71), channel_id=1, source_target_pairs={{0,64},{64,128},{128,192},{192,256},{256,320},{320,384},{384,448},... | collective-permute-start | bytes 393224 | tf_op jit(solution)/shard_map/while/body/eval_jaxpr/ppermute | solution.py:18
  92.7 8.4 %collective-permute-start = (bf16[32,2048]{1,0:T(8,128)(2,1)S(1)}, bf16[32,2048]{1,0:T(8,128)(2,1)S(1)}, u32[]{:S(2)}, u32[]{:S(2)}) collective-permute-start(bf16[32,2048]{1,0:T(8,128)(2,1)S(1)} %fusion.71), channel_id=1, source_target_pairs={{0,64},{64,128},{128,192},{192,256},{256,320},{320,384},{384,448},... | collective-permute-start | bytes 393224 | tf_op jit(solution)/shard_map/while/body/eval_jaxpr/ppermute | solution.py:18
  103.4 8.4 %collective-permute-start = (bf16[32,2048]{1,0:T(8,128)(2,1)S(1)}, bf16[32,2048]{1,0:T(8,128)(2,1)S(1)}, u32[]{:S(2)}, u32[]{:S(2)}) collective-permute-start(bf16[32,2048]{1,0:T(8,128)(2,1)S(1)} %fusion.71), channel_id=1, source_target_pairs={{0,64},{64,128},{128,192},{192,256},{256,320},{320,384},{384,448},... | collective-permute-start | bytes 393224 | tf_op jit(solution)/shard_map/while/body/eval_jaxpr/ppermute | solution.py:18
  114.1 8.4 %collective-permute-start = (bf16[32,2048]{1,0:T(8,128)(2,1)S(1)}, bf16[32,2048]{1,0:T(8,128)(2,1)S(1)}, u32[]{:S(2)}, u32[]{:S(2)}) collective-permute-start(bf16[32,2048]{1,0:T(8,128)(2,1)S(1)} %fusion.71), channel_id=1, source_target_pairs={{0,64},{64,128},{128,192},{192,256},{256,320},{320,384},{384,448},... | collective-permute-start | bytes 393224 | tf_op jit(solution)/shard_map/while/body/eval_jaxpr/ppermute | solution.py:18
  131.2 10.5 %collective-permute-start.1 = (bf16[32,2048]{1,0:T(8,128)(2,1)S(1)}, bf16[32,2048]{1,0:T(8,128)(2,1)S(1)}, u32[]{:S(2)}, u32[]{:S(2)}) collective-permute-start(bf16[32,2048]{1,0:T(8,128)(2,1)S(1)} %fusion.81), channel_id=1, source_target_pairs={{64,0},{128,64},{192,128},{256,192},{320,256},{384,320},{448,384},... | collective-permute-start | bytes 393224 | tf_op jit(solution)/shard_map/while/body/eval_jaxpr/ppermute | solution.py:18
  147.7 8.4 %collective-permute-start.1 = (bf16[32,2048]{1,0:T(8,128)(2,1)S(1)}, bf16[32,2048]{1,0:T(8,128)(2,1)S(1)}, u32[]{:S(2)}, u32[]{:S(2)}) collective-permute-start(bf16[32,2048]{1,0:T(8,128)(2,1)S(1)} %fusion.81), channel_id=1, source_target_pairs={{64,0},{128,64},{192,128},{256,192},{320,256},{384,320},{448,384},... | collective-permute-start | bytes 393224 | tf_op jit(solution)/shard_map/while/body/eval_jaxpr/ppermute | solution.py:18
  162.1 8.0 %collective-permute-start.1 = (bf16[32,2048]{1,0:T(8,128)(2,1)S(1)}, bf16[32,2048]{1,0:T(8,128)(2,1)S(1)}, u32[]{:S(2)}, u32[]{:S(2)}) collective-permute-start(bf16[32,2048]{1,0:T(8,128)(2,1)S(1)} %fusion.81), channel_id=1, source_target_pairs={{64,0},{128,64},{192,128},{256,192},{320,256},{384,320},{448,384},... | collective-permute-start | bytes 393224 | tf_op jit(solution)/shard_map/while/body/eval_jaxpr/ppermute | solution.py:18
  176.2 8.4 %collective-permute-start.1 = (bf16[32,2048]{1,0:T(8,128)(2,1)S(1)}, bf16[32,2048]{1,0:T(8,128)(2,1)S(1)}, u32[]{:S(2)}, u32[]{:S(2)}) collective-permute-start(bf16[32,2048]{1,0:T(8,128)(2,1)S(1)} %fusion.81), channel_id=1, source_target_pairs={{64,0},{128,64},{192,128},{256,192},{320,256},{384,320},{448,384},... | collective-permute-start | bytes 393224 | tf_op jit(solution)/shard_map/while/body/eval_jaxpr/ppermute | solution.py:18
  190.6 8.4 %collective-permute-start.1 = (bf16[32,2048]{1,0:T(8,128)(2,1)S(1)}, bf16[32,2048]{1,0:T(8,128)(2,1)S(1)}, u32[]{:S(2)}, u32[]{:S(2)}) collective-permute-start(bf16[32,2048]{1,0:T(8,128)(2,1)S(1)} %fusion.81), channel_id=1, source_target_pairs={{64,0},{128,64},{192,128},{256,192},{320,256},{384,320},{448,384},... | collective-permute-start | bytes 393224 | tf_op jit(solution)/shard_map/while/body/eval_jaxpr/ppermute | solution.py:18
  205.0 8.4 %collective-permute-start.1 = (bf16[32,2048]{1,0:T(8,128)(2,1)S(1)}, bf16[32,2048]{1,0:T(8,128)(2,1)S(1)}, u32[]{:S(2)}, u32[]{:S(2)}) collective-permute-start(bf16[32,2048]{1,0:T(8,128)(2,1)S(1)} %fusion.81), channel_id=1, source_target_pairs={{64,0},{128,64},{192,128},{256,192},{320,256},{384,320},{448,384},... | collective-permute-start | bytes 393224 | tf_op jit(solution)/shard_map/while/body/eval_jaxpr/ppermute | solution.py:18
  219.4 8.4 %collective-permute-start.1 = (bf16[32,2048]{1,0:T(8,128)(2,1)S(1)}, bf16[32,2048]{1,0:T(8,128)(2,1)S(1)}, u32[]{:S(2)}, u32[]{:S(2)}) collective-permute-start(bf16[32,2048]{1,0:T(8,128)(2,1)S(1)} %fusion.81), channel_id=1, source_target_pairs={{64,0},{128,64},{192,128},{256,192},{320,256},{384,320},{448,384},... | collective-permute-start | bytes 393224 | tf_op jit(solution)/shard_map/while/body/eval_jaxpr/ppermute | solution.py:18
  233.9 8.4 %collective-permute-start.1 = (bf16[32,2048]{1,0:T(8,128)(2,1)S(1)}, bf16[32,2048]{1,0:T(8,128)(2,1)S(1)}, u32[]{:S(2)}, u32[]{:S(2)}) collective-permute-start(bf16[32,2048]{1,0:T(8,128)(2,1)S(1)} %fusion.81), channel_id=1, source_target_pairs={{64,0},{128,64},{192,128},{256,192},{320,256},{384,320},{448,384},... | collective-permute-start | bytes 393224 | tf_op jit(solution)/shard_map/while/body/eval_jaxpr/ppermute | solution.py:18
  248.3 8.4 %collective-permute-start.1 = (bf16[32,2048]{1,0:T(8,128)(2,1)S(1)}, bf16[32,2048]{1,0:T(8,128)(2,1)S(1)}, u32[]{:S(2)}, u32[]{:S(2)}) collective-permute-start(bf16[32,2048]{1,0:T(8,128)(2,1)S(1)} %fusion.81), channel_id=1, source_target_pairs={{64,0},{128,64},{192,128},{256,192},{320,256},{384,320},{448,384},... | collective-permute-start | bytes 393224 | tf_op jit(solution)/shard_map/while/body/eval_jaxpr/ppermute | solution.py:18
  262.7 8.4 %collective-permute-start.1 = (bf16[32,2048]{1,0:T(8,128)(2,1)S(1)}, bf16[32,2048]{1,0:T(8,128)(2,1)S(1)}, u32[]{:S(2)}, u32[]{:S(2)}) collective-permute-start(bf16[32,2048]{1,0:T(8,128)(2,1)S(1)} %fusion.81), channel_id=1, source_target_pairs={{64,0},{128,64},{192,128},{256,192},{320,256},{384,320},{448,384},... | collective-permute-start | bytes 393224 | tf_op jit(solution)/shard_map/while/body/eval_jaxpr/ppermute | solution.py:18
  277.2 8.4 %collective-permute-start.1 = (bf16[32,2048]{1,0:T(8,128)(2,1)S(1)}, bf16[32,2048]{1,0:T(8,128)(2,1)S(1)}, u32[]{:S(2)}, u32[]{:S(2)}) collective-permute-start(bf16[32,2048]{1,0:T(8,128)(2,1)S(1)} %fusion.81), channel_id=1, source_target_pairs={{64,0},{128,64},{192,128},{256,192},{320,256},{384,320},{448,384},... | collective-permute-start | bytes 393224 | tf_op jit(solution)/shard_map/while/body/eval_jaxpr/ppermute | solution.py:18
  299.7 100.7 %reduce-scatter.6.cloned.1.call-start = ((), (), s32[]{:S(2)}) async-start(), calls=%async_computation.4 | async-start | bytes 1179648 | tf_op jit(solution)/shard_map/reduce_scatter | solution.py:26
  359.7 64.1 %reduce-scatter.8.cloned.1.call-start = ((), (), s32[]{:S(2)}) async-start(), calls=%async_computation.5 | async-start | bytes 196608 | tf_op jit(solution)/shard_map/reduce_scatter | solution.py:26
  (4 other events, 13.5 us)
Sparse Core Ops, SparseCore 0:
  299.9 59.7 reduce-scatter.3
  362.5 37.8 reduce-scatter.5
  403.2 20.5 reduce-scatter.7
where the time goes:
time: 434 us; the launch traced here: 432 us
  waiting for transfers between devices  219 us (50%)
  starting transfers between devices  85.2 us (20%)
  matrix products  49.8 us (11%)
  other arithmetic  37.9 us (9%)
  local copies, waits for them, and re-layouts  25.6 us (6%)
  between operations  13.2 us (3%)
    reduce_scatter x3, waiting for transfers between devices, reduced_to_own(): pieces = lax.psum_scatter(pieces, axes[k], scatter_dimension=0, tiled=True)  124 us
    ppermute x22, waiting for transfers between devices, from_behind(): return lax.ppermute(block, axis, route)  95.4 us
    ppermute x22, starting transfers between devices, from_behind(): return lax.ppermute(block, axis, route)  85.1 us
    dynamic_update_slice x22, other arithmetic, put_row(): lax.dynamic_update_index_in_dim(buffer, jnp.where(active, value, previous...  28.5 us
    dot_general x22, matrix products, contract_last(): lax.dot_general(left, right, (((1,), (1,)), ((), ())), preferred_element_...  21.8 us
    dynamic_slice x33, local copies, waits for them, and re-layouts, put_row(): previous = lax.dynamic_index_in_dim(buffer, micro_slot, 0, keepdims=False)  18.6 us
    dot_general x11, matrix products, backward_tick(): grad_hidden = jnp.dot(cotangent, weight, preferred_element_type=jnp.float32)  11.8 us
    dot_general x2, matrix products, contract_rows(): lax.dot_general(left, right, (((0,), (0,)), ((), ())), preferred_element_...  9.19 us
  transfers between devices with their start and end apart: 25, of which 25 were waited for; matrix products, arithmetic and copies ran while one was open for 0% of the time, Pallas kernels for 0%

commit v1 on v0

v1 whole, which is shorter than its diff:
```python
import functools
import math

import jax
import jax.numpy as jnp
from jax import lax
from jax.experimental import pallas as pl
from jax.experimental.pallas import tpu as pltpu
from jax.sharding import Mesh
from jax.sharding import PartitionSpec as P

DP = ("dp_0", "dp_1", "dp_2")
MESH = pl.DeviceIdType.MESH
EPSILON = 1e-05
STEP_ROWS = 16

f32 = jnp.float32
bf16 = jnp.bfloat16


def across_rows(left, right):
    return lax.dot_general(left, right, (((0,), (0,)), ((), ())), preferred_element_type=f32)


def kernel(
    factor,
    tiles,
    neighbours,
    distances,
    table_hbm,
    proj,
    upstream,
    out,
    table,
    weight,
    flip,
    stage,
    ahead,
    behind,
    inv_rms,
    cols,
    acts,
    partial,
    z_in,
    y_out,
    y_in,
    ahead_send,
    ahead_recv,
    behind_send,
    behind_recv,
    x_send,
    x_recv,
    z_send,
    z_recv,
    y_send,
    y_recv,
    load_sem,
):
    sections = lax.axis_size("section")
    xs, ys, zs = (lax.axis_size(a) for a in DP)
    section = lax.axis_index("section")
    x, y, z = (lax.axis_index(a) for a in DP)
    rows, width = upstream.shape
    micro, near, points = neighbours.shape
    steps = rows // STEP_ROWS
    slab = width // xs
    first, last = section == 0, section == sections - 1

    load_weight = pltpu.make_async_copy(proj.at[0], weight, load_sem.at[0])
    load_table = pltpu.make_async_copy(table_hbm, table, load_sem.at[1])
    load_upstream = pltpu.make_async_copy(
        upstream, stage.at[pl.ds(rows, rows)], load_sem.at[2]
    )
    load_weight.start()

    @pl.when(first)
    def _():
        load_table.start()

    @pl.when(last)
    def _():
        load_upstream.start()

    barrier = pltpu.get_barrier_semaphore()

    def greet(where):
        pl.semaphore_signal(barrier, inc=1, device_id=where, device_id_type=MESH)

    @pl.when(jnp.logical_not(first))
    def _():
        greet({"section": section - 1})

    @pl.when(jnp.logical_not(last))
    def _():
        greet({"section": section + 1})

    for d in range(1, xs):
        greet({"dp_0": lax.rem(x + d, xs)})
    for d in range(1, ys):
        greet({"dp_1": lax.rem(y + d, ys)})
    for d in range(1, zs):
        greet({"dp_2": lax.rem(z + d, zs)})

    @pl.when(first)
    def _():
        nodes = lax.broadcasted_iota(jnp.int32, (table.shape[0], points), 0)
        load_table.wait()
        for i in range(micro):
            r = distances[i]
            kernel_values = (1.0 - r) ** 3 * (1.0 + 3.0 * r)
            total = jnp.sum(kernel_values, axis=0, keepdims=True)
            index = tiles[i : i + 1, :] + neighbours[i]
            selector = jnp.zeros(nodes.shape, f32)
            for k in range(near):
                selector += jnp.where(index[k : k + 1] == nodes, kernel_values[k : k + 1], 0.0)
            selector = selector / total
            high = selector.astype(bf16)
            low = (selector - high.astype(f32)).astype(bf16)
            mixed = across_rows(high, table[...]) + across_rows(low, table[...])
            stage[i * points : (i + 1) * points, :] = mixed.astype(bf16)

    @pl.when(last)
    def _():
        load_upstream.wait()

    load_weight.wait()
    flip[...] = weight[...].T

    ends = jnp.where(jnp.logical_or(first, last), 1, 2)
    pl.semaphore_wait(barrier, xs + ys + zs - 3 + ends)

    def block(m, base=0):
        return pl.ds(pl.multiple_of(base + m * STEP_ROWS, STEP_ROWS), STEP_ROWS)

    def to_ahead(src, dst, sem):
        return pltpu.make_async_remote_copy(
            src_ref=src,
            dst_ref=dst,
            send_sem=ahead_send,
            recv_sem=sem,
            device_id={"section": lax.rem(section + 1, sections)},
            device_id_type=MESH,
        )

    def to_behind(src, dst, sem):
        return pltpu.make_async_remote_copy(
            src_ref=src,
            dst_ref=dst,
            send_sem=behind_send,
            recv_sem=sem,
            device_id={"section": lax.rem(section + sections - 1, sections)},
            device_id_type=MESH,
        )

    def ahead_copy(m):
        return to_ahead(ahead.at[block(m)], stage.at[block(m)], ahead_recv.at[m])

    def behind_copy(m):
        return to_behind(behind.at[block(m)], stage.at[block(m, rows)], behind_recv.at[m])

    def x_copy(kind, d, src, dst):
        return pltpu.make_async_remote_copy(
            src_ref=src,
            dst_ref=dst,
            send_sem=x_send.at[kind, d - 1],
            recv_sem=x_recv.at[kind, d - 1],
            device_id={"dp_0": lax.rem(x + d, xs)},
            device_id_type=MESH,
        )

    def share(m, half, act_half):
        for d in range(1, xs):
            to = lax.rem(x + d, xs)
            lanes = pl.ds(pl.multiple_of(to * slab, slab), slab)
            x_copy(
                2 * half,
                d,
                stage.at[block(m, half * rows), lanes],
                cols.at[block(m, (2 * d + half) * rows)],
            ).start()
            x_copy(
                2 * half + 1,
                d,
                acts.at[block(m, act_half * rows)],
                acts.at[block(m, (2 * d + act_half) * rows)],
            ).start()

    def forward(m):
        @pl.when(jnp.logical_not(first))
        def _():
            ahead_copy(m).wait_recv()

        stream = stage[block(m), :].astype(f32)
        inv = lax.rsqrt(jnp.mean(stream * stream, axis=-1, keepdims=True) + EPSILON)
        inner = jnp.dot(stage[block(m), :], weight[...], preferred_element_type=f32)
        hidden = jnp.tanh(inner * inv).astype(bf16)
        acts[block(m, rows), :] = hidden
        inv_rms[block(m), :] = jnp.broadcast_to(inv, (STEP_ROWS, 128))

        @pl.when(jnp.logical_not(last))
        def _():
            grown = stream + jnp.dot(hidden, flip[...], preferred_element_type=f32)
            ahead[block(m), :] = grown.astype(bf16)
            ahead_copy(m).start()

        share(m, 0, 1)

    def backward(m):
        @pl.when(jnp.logical_not(last))
        def _():
            behind_copy(m).wait_recv()

        cot = stage[block(m, rows), :]
        hidden = acts[block(m, rows), :].astype(f32)
        inv = inv_rms[block(m), 0:1]
        act_grad = jnp.dot(cot, weight[...], preferred_element_type=f32) * (1.0 - hidden * hidden)
        acts[block(m), :] = (act_grad * inv).astype(bf16)

        @pl.when(jnp.logical_not(first))
        def _():
            norm_grad = jnp.dot(act_grad.astype(bf16), flip[...], preferred_element_type=f32)
            wide = stage[block(m), :].astype(f32) * inv
            correction = jnp.mean(norm_grad * wide, axis=-1, keepdims=True)
            shrunk = cot.astype(f32) + inv * (norm_grad - wide * correction)
            behind[block(m), :] = shrunk.astype(bf16)
            behind_copy(m).start()

        share(m, 1, 0)

    lead = jnp.where(last, 1, jnp.where(section == sections - 2, 3, steps))

    def tick(t, carry):
        k = t - lead
        middle = jnp.logical_and(t >= lead, t < 2 * steps - lead)
        odd = lax.rem(k + 2 * steps, 2) == 1
        half = lax.div(k + 2 * steps, 2) - steps
        is_forward = jnp.logical_or(t < lead, jnp.logical_and(middle, odd))
        m_forward = jnp.where(t < lead, t, lead + half)
        m_backward = jnp.where(middle, half, t - steps)

        @pl.when(is_forward)
        def _():
            forward(m_forward)

        @pl.when(jnp.logical_not(is_forward))
        def _():
            backward(m_backward)

        return carry

    lax.fori_loop(0, 2 * steps, tick, 0)

    own = pl.ds(pl.multiple_of(x * slab, slab), slab)
    cols[0 : 2 * rows, :] = stage[:, own]

    def shared(kind, d):
        part = pl.ds((2 * d + (kind // 2 if kind % 2 == 0 else 1 - kind // 2)) * rows, rows)
        buffer = cols if kind % 2 == 0 else acts
        return x_copy(kind, d, buffer.at[part], buffer.at[part])

    for d in range(1, xs):
        for kind in range(4):
            shared(kind, d).wait_recv()
    local = across_rows(cols[...], acts[...])
    partial[...] = local.astype(bf16).reshape(partial.shape)

    def z_copy(d):
        to = lax.rem(z + d, zs)
        return pltpu.make_async_remote_copy(
            src_ref=partial.at[:, to],
            dst_ref=z_in.at[d - 1],
            send_sem=z_send.at[d - 1],
            recv_sem=z_recv.at[d - 1],
            device_id={"dp_2": to},
            device_id_type=MESH,
        )

    for d in range(1, zs):
        z_copy(d).start()
    summed = partial[:, z].astype(f32)
    for d in range(1, zs):
        z_copy(d).wait_recv()
        summed = summed + z_in[d - 1].astype(f32)
    y_out[...] = summed.astype(bf16)

    other = 1 - y
    y_copy = pltpu.make_async_remote_copy(
        src_ref=y_out.at[other],
        dst_ref=y_in,
        send_sem=y_send,
        recv_sem=y_recv,
        device_id={"dp_1": other},
        device_id_type=MESH,
    )
    y_copy.start()
    y_copy.wait_recv()
    out[0] = (y_out[y].astype(f32) + y_in[...].astype(f32)) * factor

    y_copy.wait_send()
    for d in range(1, zs):
        z_copy(d).wait_send()
    for d in range(1, xs):
        for kind in range(4):
            shared(kind, d).wait_send()

    @pl.when(jnp.logical_not(last))
    def _():
        to_ahead(ahead, stage.at[pl.ds(0, rows)], ahead_recv.at[0]).wait_send()

    @pl.when(jnp.logical_not(first))
    def _():
        to_behind(behind, stage.at[pl.ds(rows, rows)], behind_recv.at[0]).wait_send()


def on_device(node_table, tiles, neighbours, distances, proj, upstream):
    micro, points = tiles.shape
    rows = micro * points
    _, width, rank = proj.shape
    xs, ys, zs = (lax.axis_size(a) for a in DP)
    steps = rows // STEP_ROWS
    share = width // (xs * ys * zs)
    vmem = pl.BlockSpec(memory_space=pltpu.VMEM)
    hbm = pl.BlockSpec(memory_space=pltpu.HBM)
    dma = pltpu.SemaphoreType.DMA
    return pl.pallas_call(
        functools.partial(kernel, 1.0 / math.sqrt(rows * xs * ys * zs)),
        out_shape=jax.ShapeDtypeStruct((1, share, rank), f32),
        in_specs=[vmem] * 3 + [hbm] * 3,
        out_specs=vmem,
        scratch_shapes=[
            pltpu.VMEM(node_table.shape, bf16),
            pltpu.VMEM((width, rank), bf16),
            pltpu.VMEM((rank, width), bf16),
            pltpu.VMEM((2 * rows, width), bf16),
            pltpu.VMEM((rows, width), bf16),
            pltpu.VMEM((rows, width), bf16),
            pltpu.VMEM((rows, 128), f32),
            pltpu.VMEM((2 * xs * rows, width // xs), bf16),
            pltpu.VMEM((2 * xs * rows, rank), bf16),
            pltpu.VMEM((ys, zs, share, rank), bf16),
            pltpu.VMEM((zs - 1, ys, share, rank), bf16),
            pltpu.VMEM((ys, share, rank), bf16),
            pltpu.VMEM((share, rank), bf16),
            dma,
            dma((steps,)),
            dma,
            dma((steps,)),
            dma((4, xs - 1)),
            dma((4, xs - 1)),
            dma((zs - 1,)),
            dma((zs - 1,)),
            dma,
            dma,
            dma((3,)),
        ],
        compiler_params=pltpu.CompilerParams(
            collective_id=0, has_side_effects=True
        ),
    )(
        tiles,
        neighbours.transpose(0, 2, 1),
        distances.transpose(0, 2, 1),
        node_table,
        proj,
        upstream.reshape(rows, width),
    )


def solution(mesh):
    finer = Mesh(
        mesh.devices.reshape(mesh.shape["section"], 4, 2, 8), ("section", "dp_0", "dp_1", "dp_2")
    )
    in_specs = (
        P(),
        P(None, DP),
        P(None, DP, None),
        P(None, DP, None),
        P("section", None, None),
        P(None, DP, None),
    )
    out_specs = P("section", DP, None)
    return jax.shard_map(
        on_device, mesh=finer, in_specs=in_specs, out_specs=out_specs, check_vma=False
    )
```

time: 434 us -> 103 us (0.24)
  waiting for transfers between devices: 219 us -> 0 us
  Pallas kernels: 0 us -> 100 us
  starting transfers between devices: 85.2 us -> 0 us
  matrix products: 49.8 us -> 0 us
  other arithmetic: 37.9 us -> 0 us
  local copies, waits for them, and re-layouts: 25.6 us -> 1.47 us
  between operations: 13.2 us -> 0.01 us
    reduce_scatter x3 -> x0, waiting for transfers between devices: 124 us -> none  [reduced_to_own(): pieces = lax.psum_scatter(pieces, axes[k], scatter_dimension=0, tiled=True)]
    pallas_call x0 -> x1, Pallas kernels: none -> 100 us  [on_device(): pl.pallas_call(functools.partial(kernel, 1.0 / math.sqrt(rows * xs * ys *...]
    ppermute x22 -> x0, waiting for transfers between devices: 95.4 us -> none  [from_behind(): return lax.ppermute(block, axis, route)]
    ppermute x22 -> x0, starting transfers between devices: 85.1 us -> none  [from_behind(): return lax.ppermute(block, axis, route)]
    dot_general x48 -> x0, matrix products: 49.8 us -> none  [the longest x22 21.8 us: contract_last(): lax.dot_general(left, right, (((1,), (1,)), ((), ())), preferred_element_...]
    dynamic_update_slice x22 -> x0, other arithmetic: 28.5 us -> none  [put_row(): lax.dynamic_update_index_in_dim(buffer, jnp.where(active, value, previous...]
    dynamic_slice x33 -> x0, local copies, waits for them, and re-layouts: 18.6 us -> none  [put_row(): previous = lax.dynamic_index_in_dim(buffer, micro_slot, 0, keepdims=False)]
    transpose x1 -> x0, local copies, waits for them, and re-layouts: 4.97 us -> none  [reduced_to_own(): pieces = jnp.moveaxis(pieces, turns, range(len(axes))).reshape(-1, *inside)]
  transfers between devices with their start and end apart: 25 -> 0, of which waited for: 25 -> 0; matrix products, arithmetic and copies ran while one was open for 0% -> 0% of each run, Pallas kernels for 0% -> 0%
where the time goes in v1:
time: 103 us; the launch traced here: 102 us
  Pallas kernels  100 us (97%)
  local copies, waits for them, and re-layouts  1.47 us (1%)
    pallas_call x1, Pallas kernels, on_device(): pl.pallas_call(functools.partial(kernel, 1.0 / math.sqrt(rows * xs * ys *...  100 us

profile of v1, /device:TPU:1, one launch (start us, length us, event | category | flops | bytes accessed | tf_op | source)
XLA Modules:
  0.0 101.5 jit_solution(15917062351630545885)
XLA Ops:
  0.0 100.0 %shard_map.64 = f32[1,32,512]{2,1,0:T(8,128)} custom-call(s32[4,32]{1,0:T(4,128)} %tiles.1, s32[4,8,32]{2,1,0:T(8,128)} %bitcast.4, f32[4,8,32]{2,1,0:T(8,128)} %bitcast.5, bf16[128,2048]{1,0:T(8,128)(2,1)} %table_hbm.1, bf16[1,2048,512]{2,1,0:T(8,128)(2,1)} %proj.1, bf16[128,2048]{1,0:T(8,128)(2,1)} %bitcast.3), custom_call_target="tpu_custom_call" | custom-call | tf_op jit(solution)/shard_map/pallas_call | solution.py:325
  100.0 1.5 %copy.8 = f32[1,32,512]{2,1,0:T(8,128)} copy(f32[1,32,512]{2,1,0:T(8,128)} %shard_map.64) | data formatting | bytes 131072

commit v2 on v1

--- a/solution.py
+++ b/solution.py
@@ -41,19 +41,15 @@
     cols,
     acts,
     partial,
-    z_in,
-    y_out,
-    y_in,
+    arrived,
     ahead_send,
     ahead_recv,
     behind_send,
     behind_recv,
     x_send,
     x_recv,
-    z_send,
-    z_recv,
-    y_send,
-    y_recv,
+    plane_send,
+    plane_recv,
     load_sem,
 ):
     sections = lax.axis_size("section")
@@ -96,10 +92,14 @@
 
     for d in range(1, xs):
         greet({"dp_0": lax.rem(x + d, xs)})
-    for d in range(1, ys):
-        greet({"dp_1": lax.rem(y + d, ys)})
-    for d in range(1, zs):
-        greet({"dp_2": lax.rem(z + d, zs)})
+    place = y * zs + z
+
+    def plane(d):
+        to = lax.rem(place + d, ys * zs)
+        return to, {"dp_1": lax.div(to, zs), "dp_2": lax.rem(to, zs)}
+
+    for d in range(1, ys * zs):
+        greet(plane(d)[1])
 
     @pl.when(first)
     def _():
@@ -127,7 +127,7 @@
     flip[...] = weight[...].T
 
     ends = jnp.where(jnp.logical_or(first, last), 1, 2)
-    pl.semaphore_wait(barrier, xs + ys + zs - 3 + ends)
+    pl.semaphore_wait(barrier, xs + ys * zs - 2 + ends)
 
     def block(m, base=0):
         return pl.ds(pl.multiple_of(base + m * STEP_ROWS, STEP_ROWS), STEP_ROWS)
@@ -201,6 +201,11 @@
         def _():
             grown = stream + jnp.dot(hidden, flip[...], preferred_element_type=f32)
             ahead[block(m), :] = grown.astype(bf16)
+
+            @pl.when(m > 0)
+            def _():
+                ahead_copy(m - 1).wait_send()
+
             ahead_copy(m).start()
 
         share(m, 0, 1)
@@ -223,6 +228,11 @@
             correction = jnp.mean(norm_grad * wide, axis=-1, keepdims=True)
             shrunk = cot.astype(f32) + inv * (norm_grad - wide * correction)
             behind[block(m), :] = shrunk.astype(bf16)
+
+            @pl.when(m > 0)
+            def _():
+                behind_copy(m - 1).wait_send()
+
             behind_copy(m).start()
 
         share(m, 1, 0)
@@ -264,52 +274,38 @@
     local = across_rows(cols[...], acts[...])
     partial[...] = local.astype(bf16).reshape(partial.shape)
 
-    def z_copy(d):
-        to = lax.rem(z + d, zs)
+    def plane_copy(d):
+        to, device = plane(d)
         return pltpu.make_async_remote_copy(
-            src_ref=partial.at[:, to],
-            dst_ref=z_in.at[d - 1],
-            send_sem=z_send.at[d - 1],
-            recv_sem=z_recv.at[d - 1],
-            device_id={"dp_2": to},
+            src_ref=partial.at[to],
+            dst_ref=arrived.at[d - 1],
+            send_sem=plane_send.at[d - 1],
+            recv_sem=plane_recv.at[d - 1],
+            device_id=device,
             device_id_type=MESH,
         )
 
-    for d in range(1, zs):
-        z_copy(d).start()
-    summed = partial[:, z].astype(f32)
-    for d in range(1, zs):
-        z_copy(d).wait_recv()
-        summed = summed + z_in[d - 1].astype(f32)
-    y_out[...] = summed.astype(bf16)
-
-    other = 1 - y
-    y_copy = pltpu.make_async_remote_copy(
-        src_ref=y_out.at[other],
-        dst_ref=y_in,
-        send_sem=y_send,
-        recv_sem=y_recv,
-        device_id={"dp_1": other},
-        device_id_type=MESH,
-    )
-    y_copy.start()
-    y_copy.wait_recv()
-    out[0] = (y_out[y].astype(f32) + y_in[...].astype(f32)) * factor
-
-    y_copy.wait_send()
-    for d in range(1, zs):
-        z_copy(d).wait_send()
+    for d in range(1, ys * zs):
+        plane_copy(d).start()
+    summed = partial[place].astype(f32)
+    for d in range(1, ys * zs):
+        plane_copy(d).wait_recv()
+        summed = summed + arrived[d - 1].astype(f32)
+    out[0] = summed * factor
+
+    for d in range(1, ys * zs):
+        plane_copy(d).wait_send()
     for d in range(1, xs):
         for kind in range(4):
             shared(kind, d).wait_send()
 
     @pl.when(jnp.logical_not(last))
     def _():
-        to_ahead(ahead, stage.at[pl.ds(0, rows)], ahead_recv.at[0]).wait_send()
+        ahead_copy(steps - 1).wait_send()
 
     @pl.when(jnp.logical_not(first))
     def _():
-        to_behind(behind, stage.at[pl.ds(rows, rows)], behind_recv.at[0]).wait_send()
+        behind_copy(steps - 1).wait_send()
 
 
 def on_device(node_table, tiles, neighbours, distances, proj, upstream):
@@ -337,20 +333,16 @@
             pltpu.VMEM((rows, 128), f32),
             pltpu.VMEM((2 * xs * rows, width // xs), bf16),
             pltpu.VMEM((2 * xs * rows, rank), bf16),
-            pltpu.VMEM((ys, zs, share, rank), bf16),
-            pltpu.VMEM((zs - 1, ys, share, rank), bf16),
-            pltpu.VMEM((ys, share, rank), bf16),
-            pltpu.VMEM((share, rank), bf16),
+            pltpu.VMEM((ys * zs, share, rank), bf16),
+            pltpu.VMEM((ys * zs - 1, share, rank), bf16),
             dma,
             dma((steps,)),
             dma,
             dma((steps,)),
             dma((4, xs - 1)),
             dma((4, xs - 1)),
-            dma((zs - 1,)),
-            dma((zs - 1,)),
-            dma,
-            dma,
+            dma((ys * zs - 1,)),
+            dma((ys * zs - 1,)),
             dma((3,)),
         ],
         compiler_params=pltpu.CompilerParams(

time: 103 us -> 90.3 us (0.88); the launches traced: 102 us -> 90 us
  Pallas kernels: 100 us -> 88.6 us
    pallas_call x1, Pallas kernels: 100 us -> 88.6 us  [on_device(): pl.pallas_call(functools.partial(kernel, 1.0 / math.sqrt(rows * xs * ys *...]
where the time goes in v2:
time: 90.3 us; the launch traced here: 90 us
  Pallas kernels  88.6 us (98%)
  local copies, waits for them, and re-layouts  1.47 us (2%)
    pallas_call x1, Pallas kernels, on_device(): pl.pallas_call(functools.partial(kernel, 1.0 / math.sqrt(rows * xs * ys *...  88.6 us

profile of v2, /device:TPU:1, one launch (start us, length us, event | category | flops | bytes accessed | tf_op | source)
XLA Modules:
  0.0 90.0 jit_solution(677358760913402539)
XLA Ops:
  0.0 88.6 %shard_map.64 = f32[1,32,512]{2,1,0:T(8,128)} custom-call(s32[4,32]{1,0:T(4,128)} %tiles.1, s32[4,8,32]{2,1,0:T(8,128)} %bitcast.4, f32[4,8,32]{2,1,0:T(8,128)} %bitcast.5, bf16[128,2048]{1,0:T(8,128)(2,1)} %table_hbm.1, bf16[1,2048,512]{2,1,0:T(8,128)(2,1)} %proj.1, bf16[128,2048]{1,0:T(8,128)(2,1)} %bitcast.3), custom_call_target="tpu_custom_call" | custom-call | tf_op jit(solution)/shard_map/pallas_call | solution.py:321
  88.6 1.5 %copy.8 = f32[1,32,512]{2,1,0:T(8,128)} copy(f32[1,32,512]{2,1,0:T(8,128)} %shard_map.64) | data formatting | bytes 131072
